TPU v7x, 256 devices: a whole 4x4x8 slice. The times are simulated.
256 devices in a mesh: rows: 32 (over x_lo, z, core), cols: 8 (over x_hi, y).
Axes of the slice: x: 4 (x_hi: 2, x_lo: 2; x = x_hi * 2 + x_lo), y: 4, z: 8, core: 2. Of those that a mesh axis runs over, the one named last changes fastest.
Arguments:
- rhs: float32 [65536, 16], P(('rows', 'cols')), may hold values from -6 to 6
- diagonal: float32 [65536], P(('rows', 'cols')), may hold values from 1 to 16
- blocks: float32 [512, 16, 128, 128], P('rows', 'cols'), may hold values from -0.078125 to 0.078125
- block_cols: int32 [512, 16], P('rows', 'cols'), may hold values from 0 to 63
- counts: int32 [512, 8], P('rows', 'cols'), may hold values from 1 to 2
Outputs:
- solution: float32 [65536, 16], P(('rows', 'cols'))
Inputs may be any that keep to these rules, and one draw needn't show every extreme that they name: Every entry of block_cols names a block column within its slot's group, from 0 to 63; entries may repeat within a row. `counts`: every count lies between 1 and 2; the slots past the count in a group hold blocks that are not used.
All inputs are finite; a program needn't handle non-finite values.
Results may differ from a plain program's by a relative error of at most 0.0001.
Values sent between devices are 32-bit elements; how exact they have to be, the bound alone decides.
A program may use at most 64 MiB of HBM per device.

v0:
```python
import math

import jax
import jax.numpy as jnp
from jax import lax
from jax.sharding import PartitionSpec as P

ITERS = 4


def copy_for_each(shard, axis):
    length = lax.axis_size(axis)
    return lax.all_to_all(
        jnp.broadcast_to(shard[None], (length, *shard.shape)), axis, 0, 0, tiled=True
    )


def in_order(pieces, dim):
    pieces = jnp.moveaxis(pieces, 0, dim)
    lengths = pieces.shape
    return pieces.reshape(*lengths[:dim], lengths[dim] * lengths[dim + 1], *lengths[dim + 2 :])


def gathered_copies(shard, axis, dim):
    pieces = copy_for_each(shard, axis)
    return in_order(pieces, dim)


def of_everyone(shard, axis):
    return copy_for_each(shard, axis).sum(axis=0)


def in_one_piece(arrays, axis, dim, along):
    widths = [math.prod(a.shape[along:]) for a in arrays]
    both = jnp.concatenate(
        [a.reshape(*a.shape[:along], w) for a, w in zip(arrays, widths)], axis=along
    )
    whole = lax.all_gather(both, axis, axis=dim, tiled=True)
    pieces = jnp.split(whole, [sum(widths[:k]) for k in range(1, len(widths))], axis=along)
    return tuple(
        (b.reshape(*whole.shape[:along], *a.shape[along:]) for a, b in zip(arrays, pieces))
    )


def together(arrays, axis):
    vector, at, finished = (jnp.concatenate([a.reshape(-1) for a in arrays]), 0, [])
    subtotal = of_everyone(vector, axis)
    for a in arrays:
        finished.append(subtotal[at : at + a.size].reshape(a.shape))
        at += a.size
    return tuple(finished)


def solve_block(matrix, right):
    size = matrix.shape[0]
    joined = jnp.concatenate([matrix, right], axis=1)
    for index in range(size):
        pivot_row = joined[index] / joined[index, index]
        joined = joined - joined[:, index : index + 1] * pivot_row[None, :]
        joined = joined.at[index].set(pivot_row)
    return joined[:, size:]


def gram(left, right):
    return jnp.dot(left.T, right, precision=lax.Precision.HIGHEST)


def times_block(vectors, small):
    return jnp.dot(vectors, small, precision=lax.Precision.HIGHEST)


def per_device(rhs, diagonal, blocks, block_cols, counts):
    width = blocks.shape[2]
    piece_rows = rhs.shape[0]
    used = (lax.broadcasted_iota(jnp.int32, block_cols.shape, 1) < counts).astype(jnp.float32)

    def block_rows(gathered, count):
        number = count // width
        segment = gathered.reshape(-1, width, gathered.shape[1])
        picked = segment[block_cols] * used[:, :, None, None]
        product = jnp.einsum("rkij,rkjs->ris", blocks, picked, precision=lax.Precision.HIGHEST)
        return product.reshape(number * width, gathered.shape[1])

    def product_of(piece):
        gathered = gathered_copies(piece, "rows", 0)
        total = block_rows(gathered, blocks.shape[0] * width)
        return of_everyone(total, "cols")

    start_rows, diag_rows = in_one_piece((rhs, diagonal), "cols", 0, 1)
    offset = lax.axis_index("cols") * piece_rows

    def apply(vectors):
        piece = lax.dynamic_slice_in_dim(vectors, offset, piece_rows, 0)
        return diag_rows[:, None] * vectors + product_of(piece)

    solution = jnp.zeros_like(start_rows)
    residual = start_rows
    direction = start_rows
    for iteration in range(ITERS):
        image = apply(direction)
        matrix, right = together((gram(start_rows, image), gram(start_rows, residual)), "rows")
        alpha = solve_block(matrix, right)
        middle = residual - times_block(image, alpha)
        second = apply(middle)
        along, square, cross = together(
            (jnp.sum(second * middle), jnp.sum(second * second), gram(start_rows, second)), "rows"
        )
        omega = along / square
        solution = solution + times_block(direction, alpha) + omega * middle
        residual = middle - omega * second
        beta = -solve_block(matrix, cross)
        direction = residual + times_block(direction - omega * image, beta)
    return lax.dynamic_slice_in_dim(solution, offset, piece_rows, 0)


def solution(mesh):
    in_specs = (
        P(("rows", "cols"), None),
        P(("rows", "cols")),
        P("rows", "cols", None, None),
        P("rows", "cols"),
        P("rows", "cols"),
    )
    out_specs = P(("rows", "cols"), None)
    return jax.shard_map(
        per_device, mesh=mesh, in_specs=in_specs, out_specs=out_specs, check_vma=False
    )
```

profile of v0, /device:TPU:1, one launch (start us, length us, event | category | flops | bytes accessed | tf_op | source)
XLA Modules:
  0.0 813.1 jit_solution(13670134889492838594)
XLA Ops:
  0.9 29.4 %all_gather.3 = f32[2048,17]{0,1:T(8,128)S(1)} all-gather(f32[256,17]{0,1:T(8,128)S(1)} %pad_maximum_fusion), channel_id=1, replica_groups=mesh['rows'=32,'cols'=8] {'cols'}, dimensions={0}, use_global_device_ids=true | all-gather | bytes 156672 | tf_op jit(solution)/shard_map/all_gather | solution.py:38
  31.2 15.9 %all-to-all-start = ((f32[32,256,16]{1,2,0:T(8,128)}), f32[32,256,16]{1,2,0:T(8,128)S(1)}, u32[]{:S(2)}, u32[]{:S(2)}) async-start(f32[32,256,16]{1,2,0:T(8,128)} %broadcast_in_dim.66), calls=%async_computation | async-start | bytes 1048576 | tf_op jit(solution)/shard_map/all_to_all | solution.py:13
  47.4 16.3 %all-to-all-done = f32[32,256,16]{1,2,0:T(8,128)S(1)} async-done(((f32[32,256,16]{1,2,0:T(8,128)}), f32[32,256,16]{1,2,0:T(8,128)S(1)}, u32[]{:S(2)}, u32[]{:S(2)}) %all-to-all-start) | async-done | bytes 524320 | tf_op jit(solution)/shard_map/all_to_all | solution.py:13
  66.8 1.9 convolution_bitcast_fusion.7
  69.8 6.2 all-to-all-start.1
  76.4 12.5 %all-to-all-done.1 = f32[8,2048,16]{1,2,0:T(8,128)S(1)} async-done(((f32[8,2048,16]{1,2,0:T(8,128)}), f32[8,2048,16]{1,2,0:T(8,128)S(1)}, u32[]{:S(2)}, u32[]{:S(2)}) %all-to-all-start.1) | async-done | bytes 1048608 | tf_op jit(solution)/shard_map/all_to_all | solution.py:13
  89.3 15.1 %all_to_all.128 = f32[32,1,512]{2,1,0:T(1,128)S(1)} all-to-all(f32[32,1,512]{2,1,0:T(1,128)S(1)} %broadcast_in_dim.70), channel_id=1, replica_groups=mesh['rows'=32,'cols'=8] {'rows'}, dimensions={0} | all-to-all | bytes 131072 | tf_op jit(solution)/shard_map/all_to_all | solution.py:13
  142.9 20.6 %all_to_all.129 = f32[32,256,16]{1,2,0:T(8,128)S(1)} all-to-all(f32[32,256,16]{1,2,0:T(8,128)S(1)} %broadcast_in_dim.71), channel_id=1, replica_groups=mesh['rows'=32,'cols'=8] {'rows'}, dimensions={0} | all-to-all | bytes 1048576 | tf_op jit(solution)/shard_map/all_to_all | solution.py:13
  166.5 1.9 convolution_bitcast_fusion.6
  168.5 18.7 %all_to_all.130 = f32[8,2048,16]{1,2,0:T(8,128)S(1)} all-to-all(f32[8,2048,16]{1,2,0:T(8,128)S(1)} %broadcast_in_dim.73), channel_id=1, replica_groups=mesh['rows'=32,'cols'=8] {'cols'}, dimensions={0} | all-to-all | bytes 2097152 | tf_op jit(solution)/shard_map/all_to_all | solution.py:13
  188.0 1.6 multiply_reduce_fusion.7
  192.3 15.1 %all_to_all.131 = f32[32,1,258]{2,1,0:T(1,128)S(1)} all-to-all(f32[32,1,258]{2,1,0:T(1,128)S(1)} %broadcast_in_dim.74), channel_id=1, replica_groups=mesh['rows'=32,'cols'=8] {'rows'}, dimensions={0} | all-to-all | bytes 66048 | tf_op jit(solution)/shard_map/all_to_all | solution.py:13
  246.3 20.4 %all_to_all.132 = f32[32,256,16]{1,2,0:T(8,128)S(1)} all-to-all(f32[32,256,16]{1,2,0:T(8,128)S(1)} %broadcast_in_dim.75), channel_id=1, replica_groups=mesh['rows'=32,'cols'=8] {'rows'}, dimensions={0} | all-to-all | bytes 1048576 | tf_op jit(solution)/shard_map/all_to_all | solution.py:13
  269.8 1.9 convolution_bitcast_fusion.5
  272.8 3.6 all-to-all-start.7
  277.7 11.8 %all-to-all-done.7 = f32[8,2048,16]{1,2,0:T(8,128)S(1)} async-done(((f32[8,2048,16]{1,2,0:T(8,128)}), f32[8,2048,16]{1,2,0:T(8,128)S(1)}, u32[]{:S(2)}, u32[]{:S(2)}) %all-to-all-start.7) | async-done | bytes 1048608 | tf_op jit(solution)/shard_map/all_to_all | solution.py:13
  291.6 15.5 %all_to_all.133 = f32[32,1,512]{2,1,0:T(1,128)S(1)} all-to-all(f32[32,1,512]{2,1,0:T(1,128)S(1)} %broadcast_in_dim.78), channel_id=1, replica_groups=mesh['rows'=32,'cols'=8] {'rows'}, dimensions={0} | all-to-all | bytes 131072 | tf_op jit(solution)/shard_map/all_to_all | solution.py:13
  341.7 1.4 convolution_subtract_fusion.2
  343.8 20.6 %all_to_all.134 = f32[32,256,16]{1,2,0:T(8,128)S(1)} all-to-all(f32[32,256,16]{1,2,0:T(8,128)S(1)} %broadcast_in_dim.79), channel_id=1, replica_groups=mesh['rows'=32,'cols'=8] {'rows'}, dimensions={0} | all-to-all | bytes 1048576 | tf_op jit(solution)/shard_map/all_to_all | solution.py:13
  367.5 1.9 convolution_bitcast_fusion.4
  369.5 18.6 %all_to_all.135 = f32[8,2048,16]{1,2,0:T(8,128)S(1)} all-to-all(f32[8,2048,16]{1,2,0:T(8,128)S(1)} %broadcast_in_dim.81), channel_id=1, replica_groups=mesh['rows'=32,'cols'=8] {'cols'}, dimensions={0} | all-to-all | bytes 2097152 | tf_op jit(solution)/shard_map/all_to_all | solution.py:13
  388.8 1.7 multiply_reduce_fusion.5
  393.2 15.1 %all_to_all.136 = f32[32,1,258]{2,1,0:T(1,128)S(1)} all-to-all(f32[32,1,258]{2,1,0:T(1,128)S(1)} %broadcast_in_dim.82), channel_id=1, replica_groups=mesh['rows'=32,'cols'=8] {'rows'}, dimensions={0} | all-to-all | bytes 66048 | tf_op jit(solution)/shard_map/all_to_all | solution.py:13
  447.5 20.4 %all_to_all.137 = f32[32,256,16]{1,2,0:T(8,128)S(1)} all-to-all(f32[32,256,16]{1,2,0:T(8,128)S(1)} %broadcast_in_dim.83), channel_id=1, replica_groups=mesh['rows'=32,'cols'=8] {'rows'}, dimensions={0} | all-to-all | bytes 1048576 | tf_op jit(solution)/shard_map/all_to_all | solution.py:13
  471.0 1.9 convolution_bitcast_fusion.3
  474.0 3.6 all-to-all-start.13
  478.8 11.8 %all-to-all-done.13 = f32[8,2048,16]{1,2,0:T(8,128)S(1)} async-done(((f32[8,2048,16]{1,2,0:T(8,128)}), f32[8,2048,16]{1,2,0:T(8,128)S(1)}, u32[]{:S(2)}, u32[]{:S(2)}) %all-to-all-start.13) | async-done | bytes 1048608 | tf_op jit(solution)/shard_map/all_to_all | solution.py:13
  492.7 15.5 %all_to_all.138 = f32[32,1,512]{2,1,0:T(1,128)S(1)} all-to-all(f32[32,1,512]{2,1,0:T(1,128)S(1)} %broadcast_in_dim.86), channel_id=1, replica_groups=mesh['rows'=32,'cols'=8] {'rows'}, dimensions={0} | all-to-all | bytes 131072 | tf_op jit(solution)/shard_map/all_to_all | solution.py:13
  543.4 1.4 convolution_subtract_fusion.1
  545.6 20.6 %all_to_all.139 = f32[32,256,16]{1,2,0:T(8,128)S(1)} all-to-all(f32[32,256,16]{1,2,0:T(8,128)S(1)} %broadcast_in_dim.87), channel_id=1, replica_groups=mesh['rows'=32,'cols'=8] {'rows'}, dimensions={0} | all-to-all | bytes 1048576 | tf_op jit(solution)/shard_map/all_to_all | solution.py:13
  569.2 1.9 convolution_bitcast_fusion.2
  571.2 18.6 %all_to_all.140 = f32[8,2048,16]{1,2,0:T(8,128)S(1)} all-to-all(f32[8,2048,16]{1,2,0:T(8,128)S(1)} %broadcast_in_dim.89), channel_id=1, replica_groups=mesh['rows'=32,'cols'=8] {'cols'}, dimensions={0} | all-to-all | bytes 2097152 | tf_op jit(solution)/shard_map/all_to_all | solution.py:13
  590.5 1.7 multiply_reduce_fusion.3
  594.9 15.1 %all_to_all.141 = f32[32,1,258]{2,1,0:T(1,128)S(1)} all-to-all(f32[32,1,258]{2,1,0:T(1,128)S(1)} %broadcast_in_dim.90), channel_id=1, replica_groups=mesh['rows'=32,'cols'=8] {'rows'}, dimensions={0} | all-to-all | bytes 66048 | tf_op jit(solution)/shard_map/all_to_all | solution.py:13
  646.3 1.4 convolution_add_fusion
  648.3 20.4 %all_to_all.142 = f32[32,256,16]{1,2,0:T(8,128)S(1)} all-to-all(f32[32,256,16]{1,2,0:T(8,128)S(1)} %broadcast_in_dim.91), channel_id=1, replica_groups=mesh['rows'=32,'cols'=8] {'rows'}, dimensions={0} | all-to-all | bytes 1048576 | tf_op jit(solution)/shard_map/all_to_all | solution.py:13
  671.8 1.9 convolution_bitcast_fusion.1
  674.8 3.6 all-to-all-start.19
  679.7 11.8 %all-to-all-done.19 = f32[8,2048,16]{1,2,0:T(8,128)S(1)} async-done(((f32[8,2048,16]{1,2,0:T(8,128)}), f32[8,2048,16]{1,2,0:T(8,128)S(1)}, u32[]{:S(2)}, u32[]{:S(2)}) %all-to-all-start.19) | async-done | bytes 1048608 | tf_op jit(solution)/shard_map/all_to_all | solution.py:13
  693.6 15.5 %all_to_all.143 = f32[32,1,512]{2,1,0:T(1,128)S(1)} all-to-all(f32[32,1,512]{2,1,0:T(1,128)S(1)} %broadcast_in_dim.94), channel_id=1, replica_groups=mesh['rows'=32,'cols'=8] {'rows'}, dimensions={0} | all-to-all | bytes 131072 | tf_op jit(solution)/shard_map/all_to_all | solution.py:13
  743.7 1.4 convolution_subtract_fusion
  745.2 20.6 %all_to_all.144 = f32[32,256,16]{1,2,0:T(8,128)S(1)} all-to-all(f32[32,256,16]{1,2,0:T(8,128)S(1)} %broadcast_in_dim.95), channel_id=1, replica_groups=mesh['rows'=32,'cols'=8] {'rows'}, dimensions={0} | all-to-all | bytes 1048576 | tf_op jit(solution)/shard_map/all_to_all | solution.py:13
  768.8 1.9 convolution_bitcast_fusion
  771.9 4.7 all-to-all-start.22
  777.7 11.8 %all-to-all-done.22 = f32[8,2048,16]{1,2,0:T(8,128)} async-done(((f32[8,2048,16]{1,2,0:T(8,128)}), f32[8,2048,16]{1,2,0:T(8,128)}, u32[]{:S(2)}, u32[]{:S(2)}) %all-to-all-start.22) | async-done | bytes 1048608 | tf_op jit(solution)/shard_map/all_to_all | solution.py:13
  793.8 7.5 all-to-all-start.23
  801.7 7.7 all-to-all-done.23
  811.3 1.4 fusion.33
  (850 shorter events, 313.5 us)
Async XLA Ops:
  0.0 66.8 %copy-start = (f32[16,2,128,128]{3,2,1,0:T(8,128)S(1)}, f32[16,2,128,128]{3,2,1,0:T(8,128)}, u32[]{:S(2)}) copy-start(f32[16,2,128,128]{3,2,1,0:T(8,128)} %param.231) | copy-start | bytes 6291460
  0.0 47.1 %copy-start.13 = (s32[16,2]{0,1:T(2,128)S(1)}, s32[16,2]{0,1:T(2,128)}, u32[]{:S(2)}) copy-start(s32[16,2]{0,1:T(2,128)} %param.232) | copy-start | bytes 388
  0.0 47.3 %copy-start.14 = (s32[16,1]{0,1:T(1,128)S(1)}, s32[16,1]{0,1:T(1,128)}, u32[]{:S(2)}) copy-start(s32[16,1]{0,1:T(1,128)} %param.233) | copy-start | bytes 196
  31.2 32.5 %all-to-all-start = ((f32[32,256,16]{1,2,0:T(8,128)}), f32[32,256,16]{1,2,0:T(8,128)S(1)}, u32[]{:S(2)}, u32[]{:S(2)}) async-start(f32[32,256,16]{1,2,0:T(8,128)} %broadcast_in_dim.66), calls=%async_computation | async-start | bytes 1048576 | tf_op jit(solution)/shard_map/all_to_all | solution.py:13
  69.8 19.0 %all-to-all-start.1 = ((f32[8,2048,16]{1,2,0:T(8,128)}), f32[8,2048,16]{1,2,0:T(8,128)S(1)}, u32[]{:S(2)}, u32[]{:S(2)}) async-start(f32[8,2048,16]{1,2,0:T(8,128)} %broadcast_in_dim.69), calls=%async_computation.1 | async-start | bytes 2097152 | tf_op jit(solution)/shard_map/all_to_all | solution.py:13
  88.9 52.6 %copy-start.9 = (f32[2048,16]{0,1:T(8,128)}, f32[2048,16]{0,1:T(8,128)S(1)}, u32[]{:S(2)}) copy-start(f32[2048,16]{0,1:T(8,128)S(1)} %reduce_sum.216) | copy-start | bytes 393220
  244.2 2.1 copy-start.11
  245.6 0.7 copy-start.1
  272.8 16.6 %all-to-all-start.7 = ((f32[8,2048,16]{1,2,0:T(8,128)}), f32[8,2048,16]{1,2,0:T(8,128)S(1)}, u32[]{:S(2)}, u32[]{:S(2)}) async-start(f32[8,2048,16]{1,2,0:T(8,128)} %broadcast_in_dim.77), calls=%async_computation.7 | async-start | bytes 2097152 | tf_op jit(solution)/shard_map/all_to_all | solution.py:13
  343.1 0.6 copy-start.5
  445.3 2.2 copy-start.12
  446.8 0.6 copy-start.3
  474.0 16.6 %all-to-all-start.13 = ((f32[8,2048,16]{1,2,0:T(8,128)}), f32[8,2048,16]{1,2,0:T(8,128)S(1)}, u32[]{:S(2)}, u32[]{:S(2)}) async-start(f32[8,2048,16]{1,2,0:T(8,128)} %broadcast_in_dim.85), calls=%async_computation.13 | async-start | bytes 2097152 | tf_op jit(solution)/shard_map/all_to_all | solution.py:13
  544.8 0.7 copy-start.6
  645.9 2.4 copy-start.10
  647.6 0.6 copy-start.7
  674.8 16.6 %all-to-all-start.19 = ((f32[8,2048,16]{1,2,0:T(8,128)}), f32[8,2048,16]{1,2,0:T(8,128)S(1)}, u32[]{:S(2)}, u32[]{:S(2)}) async-start(f32[8,2048,16]{1,2,0:T(8,128)} %broadcast_in_dim.93), calls=%async_computation.19 | async-start | bytes 2097152 | tf_op jit(solution)/shard_map/all_to_all | solution.py:13
  770.7 6.3 copy-start.2
  770.7 6.7 copy-start.4
  771.9 29.4 %copy-start.8 = (f32[2048,16]{0,1:T(8,128)S(1)}, f32[2048,16]{0,1:T(8,128)}, u32[]{:S(2)}) copy-start(f32[2048,16]{0,1:T(8,128)} %copy-done.7) | copy-start | bytes 393220
  771.9 17.7 %all-to-all-start.22 = ((f32[8,2048,16]{1,2,0:T(8,128)}), f32[8,2048,16]{1,2,0:T(8,128)}, u32[]{:S(2)}, u32[]{:S(2)}) async-start(f32[8,2048,16]{1,2,0:T(8,128)} %broadcast_in_dim.97), calls=%async_computation.22 | async-start | bytes 2097152 | tf_op jit(solution)/shard_map/all_to_all | solution.py:13
  793.8 15.6 %all-to-all-start.23 = ((f32[32,1,258]{2,1,0:T(1,128)}), f32[32,1,258]{2,1,0:T(1,128)S(1)}, u32[]{:S(2)}, u32[]{:S(2)}) async-start(f32[32,1,258]{2,1,0:T(1,128)} %broadcast_in_dim.98), calls=%async_computation.23 | async-start | bytes 98304 | tf_op jit(solution)/shard_map/all_to_all | solution.py:13
where the time goes:
time: 826 us; the launch traced here: 813 us
  blocking collectives  336 us (41%)
  other arithmetic  170 us (21%)
  local copies, waits for them, and re-layouts  133 us (16%)
  waiting for transfers between devices  83.5 us (10%)
  starting transfers between devices  45 us (5%)
  matrix products  37.5 us (5%)
    all_to_all x17, blocking collectives, copy_for_each(): lax.all_to_all(jnp.broadcast_to(shard[None], (length, *shard.shape)), axi...  307 us
    all_to_all x7, waiting for transfers between devices, copy_for_each(): lax.all_to_all(jnp.broadcast_to(shard[None], (length, *shard.shape)), axi...  83.5 us
    div x112, other arithmetic, solve_block(): pivot_row = joined[index] / joined[index, index]  72.2 us
    slice x109, local copies, waits for them, and re-layouts, solve_block(): pivot_row = joined[index] / joined[index, index]  68.3 us
    mul x105, other arithmetic, solve_block(): joined = joined - joined[:, index:index + 1] * pivot_row[None, :]  67.2 us
    all_to_all x7, starting transfers between devices, copy_for_each(): lax.all_to_all(jnp.broadcast_to(shard[None], (length, *shard.shape)), axi...  45 us
    all_gather x1, blocking collectives, in_one_piece(): whole = lax.all_gather(both, axis, axis=dim, tiled=True)  29.4 us
    slice x109, local copies, waits for them, and re-layouts, solve_block(): joined = joined - joined[:, index:index + 1] * pivot_row[None, :]  19.5 us
  transfers between devices with their start and end apart: 7, of which 7 were waited for; matrix products, arithmetic and copies ran while one was open for 1% of the time, Pallas kernels for 0%

commit v1 on v0

v1 whole, which is shorter than its diff:
```python
import functools

import jax
import jax.numpy as jnp
from jax import lax
from jax.experimental import pallas as pl
from jax.experimental.pallas import tpu as pltpu
from jax.sharding import PartitionSpec as P

ITERS = 4
MESH = pl.DeviceIdType.MESH
HIGHEST = lax.Precision.HIGHEST
F32 = jnp.float32
BF16 = jnp.bfloat16
NT = (((1,), (1,)), ((), ()))
NN = (((1,), (0,)), ((), ()))


def mm(a, b, dims=NN):
    return lax.dot_general(a, b, dims, precision=HIGHEST, preferred_element_type=F32)


def kernel(
    sizes,
    cols_ref, counts_ref, rhs_ref, diag_ref, blocks_ref, out_ref,
    at, gb0, gb1, prod, rsb, arx, ary, arz,
    sh, pv, sv, zv, vv, rv, wv, tv, qv, xv, at_small,
    ag_ssem, ag_rsem, dd_ssem, dd_rsem, rs_ssem, rs_rsem,
    ax_ssem, ax_rsem, ay_ssem, ay_rsem, az_ssem, az_rsem,
):
    NZ, NY = sizes
    r = lax.axis_index("rows")
    c = lax.axis_index("cols")
    core = lax.rem(r, 2)
    z = lax.rem(lax.div(r, 2), NZ)
    a = lax.div(r, 2 * NZ)
    xh = lax.div(c, NY)
    y = lax.rem(c, NY)
    x = xh * 2 + a
    n_cols = 2 * NY

    def row_of(a_, z_, k_):
        return (a_ * NZ + z_) * 2 + k_

    def place(k_, a_, z_):
        return ((k_ * 2 + a_) * NZ + z_) * 2

    z_order = sorted(range(NZ), key=lambda d: -min(d, NZ - d))
    y_order = sorted(range(NY), key=lambda d: -min(d, NY - d))
    gather_peers = []
    for da in (1, 0):
        for dz in z_order:
            if (da, dz) != (0, 0):
                gather_peers.append((lax.rem(a + da, 2), lax.rem(z + dz, NZ)))
    scatter_peers = []
    for dx in (1, 0):
        for dy in y_order:
            if (dx, dy) != (0, 0):
                scatter_peers.append((lax.rem(xh + dx, 2), lax.rem(y + dy, NY)))
    partner = r + 1 - 2 * core
    plane_peers = []
    for dx in (2, 1, 3, 0):
        for dk in (1, 0):
            if (dx, dk) != (0, 0):
                plane_peers.append((lax.rem(x + dx, 4), lax.rem(core + dk, 2)))
    y_peers = [lax.rem(y + d, NY) for d in y_order if d != 0]
    z_peers = [lax.rem(z + d, NZ) for d in z_order if d != 0]

    def plane_device(x_, k_):
        return (row_of(lax.rem(x_, 2), z, k_), lax.div(x_, 2) * NY + y)

    barrier = pltpu.get_barrier_semaphore()
    greet = [(row_of(a_, z_, core), c) for a_, z_ in gather_peers]
    greet.append((partner, c))
    greet += [(r, xh_ * NY + y_) for xh_, y_ in scatter_peers]
    extra = []
    for dx in (2, 1, 3, 0):
        for dk in (1, 0):
            if (dx, dk) in ((0, 0), (2, 0), (0, 1)):
                continue
            extra.append(plane_device(lax.rem(x + dx, 4), lax.rem(core + dk, 2)))
    greet += extra
    for device in greet:
        pl.semaphore_signal(barrier, inc=1, device_id=device, device_id_type=MESH)

    def prepare(b, carry):
        cnt = counts_ref[b]
        for k in range(2):
            blk = blocks_ref[b, k]
            blk = jnp.where(k < cnt, blk, 0.0).T
            hi = blk.astype(BF16)
            mid = (blk - hi.astype(F32)).astype(BF16)
            at[b, k * 128:(k + 1) * 128, 0:128] = hi
            at[b, k * 128:(k + 1) * 128, 128:256] = mid
        return carry

    lax.fori_loop(0, 16, prepare, 0)

    rhs = rhs_ref[...]
    sh[...] = rhs
    rv[...] = rhs
    wv[...] = rhs
    zv[...] = rhs
    qv[...] = rhs
    xv[...] = -rhs
    zero = jnp.zeros_like(rhs)
    pv[...] = zero
    sv[...] = zero
    vv[...] = zero
    tv[...] = zero
    row16 = lax.broadcasted_iota(jnp.int32, (16, 128), 0)
    lane16 = lax.broadcasted_iota(jnp.int32, (16, 128), 1)
    eye_at_32 = jnp.where(lane16 == row16 + 32, 1.0, 0.0)
    row32 = lax.broadcasted_iota(jnp.int32, (32, 128), 0)
    lane32 = lax.broadcasted_iota(jnp.int32, (32, 128), 1)
    pick = jnp.where(lane32 == row32 + 16, 1.0, 0.0)
    pad96 = jnp.zeros((96, 256), F32)
    pad112 = jnp.zeros((112, 256), F32)
    at_small[...] = jnp.zeros((32, 16), F32)

    pl.semaphore_wait(barrier, len(greet))

    gbs = (gb0, gb1)

    def gather_start(par, vec):
        gb = gbs[par]
        mine = place(core, a, z)
        gb[mine] = vec[:, 0:128]
        gb[mine + 1] = vec[:, 128:256]
        sends = []
        for n, (a_, z_) in enumerate(gather_peers):
            cp = pltpu.make_async_remote_copy(
                src_ref=gb.at[pl.ds(mine, 2)],
                dst_ref=gb.at[pl.ds(mine, 2)],
                send_sem=ag_ssem.at[n],
                recv_sem=ag_rsem.at[par, a * NZ + z],
                device_id=(row_of(a_, z_, core), c),
                device_id_type=MESH,
            )
            cp.start()
            sends.append(cp)
        return sends

    def gather_finish(par):
        gb = gbs[par]
        sends = []
        for half in range(2):
            a_half = lax.rem(a + half, 2)
            for dz in reversed(z_order):
                if (half, dz) == (0, 0):
                    continue
                z_ = lax.rem(z + dz, NZ)
                there = place(core, a_half, z_)
                pltpu.make_async_remote_copy(
                    src_ref=gb.at[pl.ds(there, 2)],
                    dst_ref=gb.at[pl.ds(there, 2)],
                    send_sem=ag_ssem.at[0],
                    recv_sem=ag_rsem.at[par, a_half * NZ + z_],
                    device_id=(partner, c),
                    device_id_type=MESH,
                ).wait_recv()
            start = place(core, a_half, 0)
            cp = pltpu.make_async_remote_copy(
                src_ref=gb.at[pl.ds(start, 2 * NZ)],
                dst_ref=gb.at[pl.ds(start, 2 * NZ)],
                send_sem=dd_ssem.at[half],
                recv_sem=dd_rsem.at[par, a_half],
                device_id=(partner, c),
                device_id_type=MESH,
            )
            cp.start()
            sends.append(cp)
        for half in range(2):
            a_half = lax.rem(a + half, 2)
            start = place(1 - core, a_half, 0)
            pltpu.make_async_remote_copy(
                src_ref=gb.at[pl.ds(start, 2 * NZ)],
                dst_ref=gb.at[pl.ds(start, 2 * NZ)],
                send_sem=dd_ssem.at[half],
                recv_sem=dd_rsem.at[par, a_half],
                device_id=(partner, c),
                device_id_type=MESH,
            ).wait_recv()
        return sends

    def block_row(gb, b):
        parts = []
        for k in range(2):
            l = cols_ref[b, k]
            h = l & 1
            k_ = (l >> 1) & 1
            az = l >> 2
            parts.append(gb[((k_ * 2 * NZ + az) << 1) + h])
        v = jnp.concatenate(parts, axis=1)
        vh = v.astype(BF16)
        vm = (v - vh.astype(F32)).astype(BF16)
        both = jnp.concatenate([vh, vm], axis=0)
        full = lax.dot_general(both, at[b], NN, preferred_element_type=F32)
        return full[0:16, 0:128] + (full[16:32, 0:128] + full[0:16, 128:256])

    def products(par):
        gb = gbs[par]
        sends = []
        for n, (xh_, y_) in enumerate(scatter_peers + [(xh, y)]):
            c_ = xh_ * NY + y_
            for h in range(2):
                prod[c_, h] = block_row(gb, c_ * 2 + h)
            if n < len(scatter_peers):
                cp = pltpu.make_async_remote_copy(
                    src_ref=prod.at[c_],
                    dst_ref=rsb.at[par, c],
                    send_sem=rs_ssem.at[n],
                    recv_sem=rs_rsem.at[par, c],
                    device_id=(r, c_),
                    device_id_type=MESH,
                )
                cp.start()
                sends.append(cp)
        return sends

    def scatter_finish(par, vec):
        own = prod[c]
        total = jnp.concatenate([own[0], own[1]], axis=1) + diag_ref[...] * vec
        for xh_, y_ in reversed(scatter_peers):
            c_ = xh_ * NY + y_
            pltpu.make_async_remote_copy(
                src_ref=prod.at[c_],
                dst_ref=rsb.at[par, c_],
                send_sem=rs_ssem.at[0],
                recv_sem=rs_rsem.at[par, c_],
                device_id=(r, c_),
                device_id_type=MESH,
            ).wait_recv()
            got = rsb[par, c_]
            total = total + jnp.concatenate([got[0], got[1]], axis=1)
        return total

    def reduce_x_start(par, part):
        mine = x * 2 + core
        arx[par, mine] = part
        sends = []
        for n, (x_, k_) in enumerate(plane_peers):
            cp = pltpu.make_async_remote_copy(
                src_ref=arx.at[par, mine],
                dst_ref=arx.at[par, mine],
                send_sem=ax_ssem.at[n],
                recv_sem=ax_rsem.at[par, mine],
                device_id=plane_device(x_, k_),
                device_id_type=MESH,
            )
            cp.start()
            sends.append(cp)
        return sends

    def reduce_y_start(par):
        for x_, k_ in reversed(plane_peers):
            slot = x_ * 2 + k_
            pltpu.make_async_remote_copy(
                src_ref=arx.at[par, slot],
                dst_ref=arx.at[par, slot],
                send_sem=ax_ssem.at[0],
                recv_sem=ax_rsem.at[par, slot],
                device_id=plane_device(x_, k_),
                device_id_type=MESH,
            ).wait_recv()
        part = arx[par, 0]
        for s in range(1, 8):
            part = part + arx[par, s]
        ary[par, y] = part
        sends = []
        for n, y_ in enumerate(y_peers):
            cp = pltpu.make_async_remote_copy(
                src_ref=ary.at[par, y],
                dst_ref=ary.at[par, y],
                send_sem=ay_ssem.at[n],
                recv_sem=ay_rsem.at[par, y],
                device_id=(r, xh * NY + y_),
                device_id_type=MESH,
            )
            cp.start()
            sends.append(cp)
        return sends

    def reduce_z_start(par):
        for y_ in reversed(y_peers):
            pltpu.make_async_remote_copy(
                src_ref=ary.at[par, y_],
                dst_ref=ary.at[par, y_],
                send_sem=ay_ssem.at[0],
                recv_sem=ay_rsem.at[par, y_],
                device_id=(r, xh * NY + y_),
                device_id_type=MESH,
            ).wait_recv()
        part = ary[par, 0]
        for s in range(1, NY):
            part = part + ary[par, s]
        arz[par, z] = part
        sends = []
        for n, z_ in enumerate(z_peers):
            cp = pltpu.make_async_remote_copy(
                src_ref=arz.at[par, z],
                dst_ref=arz.at[par, z],
                send_sem=az_ssem.at[n],
                recv_sem=az_rsem.at[par, z],
                device_id=(row_of(a, z_, core), c),
                device_id_type=MESH,
            )
            cp.start()
            sends.append(cp)
        return sends

    def reduce_finish(par):
        for z_ in reversed(z_peers):
            pltpu.make_async_remote_copy(
                src_ref=arz.at[par, z_],
                dst_ref=arz.at[par, z_],
                send_sem=az_ssem.at[0],
                recv_sem=az_rsem.at[par, z_],
                device_id=(row_of(a, z_, core), c),
                device_id_type=MESH,
            ).wait_recv()
        part = arz[par, 0]
        for s in range(1, NZ):
            part = part + arz[par, s]
        return part

    def drain(sends):
        for cp in sends:
            cp.wait_send()

    def omega_part():
        yy = wv[...] - mm(at_small[0:16, :], zv[...])
        return yy

    def sums_of(yy, qq):
        d = mm(yy, jnp.concatenate([sh[...], pad112], axis=0), NT)
        along = jnp.sum(yy * qq, axis=1, keepdims=True)
        square = jnp.sum(yy * yy, axis=1, keepdims=True)
        return jnp.where(lane16 == 16, along, jnp.where(lane16 == 17, square, d))

    def omega_of(total):
        along = jnp.sum(jnp.where(lane16 == 16, total, 0.0), keepdims=True)
        square = jnp.sum(jnp.where(lane16 == 17, total, 0.0), keepdims=True)
        return along / square

    def solve(total):
        joined = jnp.where(lane16 < 32, total, eye_at_32)
        for i in range(16):
            pivot_row = joined[i:i + 1, :] / joined[i:i + 1, i:i + 1]
            column = joined[:, i:i + 1]
            joined = jnp.where(row16 == i, pivot_row, joined - column * pivot_row)
        return mm(pick, joined, NT)

    def step(i, carry):
        first = i == 0
        par = 0
        ag = gather_start(par, zv[...])
        yy = jnp.where(first, 0.0, wv[...] - mm(at_small[0:16, :], zv[...]))
        qq = qv[...]
        ax = reduce_x_start(par, sums_of(yy, qq))
        ay = reduce_y_start(par)
        az = reduce_z_start(par)
        dd = gather_finish(par)
        rs = products(par)
        total = reduce_finish(par)
        omega = jnp.where(first, 1.0, omega_of(total))
        beta_t = jnp.where(first, 0.0, -mm(total[:, 0:16], at_small[16:32, :]))
        alpha_t = at_small[0:16, :]
        xv[...] = xv[...] + mm(alpha_t, pv[...]) + omega * qq
        res = qq - omega * yy
        new_p = res + mm(beta_t, pv[...] - omega * sv[...])
        kept = mm(beta_t, sv[...] - omega * zv[...])
        left = yy - omega * tv[...]
        vv[...] = scatter_finish(par, zv[...])
        w_new = jnp.where(first, vv[...], left + omega * mm(alpha_t, vv[...]))
        drain(ag + ax + ay + az + dd + rs)
        par = 1
        ag = gather_start(par, w_new)
        s_new = w_new + kept
        d = mm(sh[...], jnp.concatenate([s_new, res, pad96], axis=0), NT)
        ax = reduce_x_start(par, d)
        wv[...] = w_new
        pv[...] = new_p
        sv[...] = s_new
        ay = reduce_y_start(par)
        az = reduce_z_start(par)
        dd = gather_finish(par)
        rs = products(par)
        total = reduce_finish(par)
        at_small[...] = solve(total)
        qv[...] = res - mm(at_small[0:16, :], s_new)
        u = mm(beta_t, zv[...] - omega * vv[...])
        t_new = scatter_finish(par, w_new)
        tv[...] = t_new
        zv[...] = jnp.where(first, t_new, t_new + u)
        drain(ag + ax + ay + az + dd + rs)
        return carry

    lax.fori_loop(0, ITERS, step, 0)

    par = 0
    qq = qv[...]
    yy = wv[...] - mm(at_small[0:16, :], zv[...])
    ax = reduce_x_start(par, sums_of(yy, qq))
    partial = xv[...] + mm(at_small[0:16, :], pv[...])
    ay = reduce_y_start(par)
    az = reduce_z_start(par)
    total = reduce_finish(par)
    out_ref[...] = partial + omega_of(total) * qq
    drain(ax + ay + az)


def per_device(sizes, rhs, diagonal, blocks, block_cols, counts):
    nz, ny = sizes
    vm = pl.BlockSpec(memory_space=pltpu.VMEM)
    sm = pl.BlockSpec(memory_space=pltpu.SMEM)
    vec = pltpu.VMEM((16, 256), F32)
    dma = pltpu.SemaphoreType.DMA
    n_ag = 2 * nz - 1
    out = pl.pallas_call(
        functools.partial(kernel, sizes),
        out_shape=jax.ShapeDtypeStruct((16, 256), F32),
        in_specs=[sm, sm, vm, vm, vm],
        out_specs=vm,
        scratch_shapes=[
            pltpu.VMEM((16, 256, 256), BF16),
            pltpu.VMEM((8 * nz, 16, 128), F32),
            pltpu.VMEM((8 * nz, 16, 128), F32),
            pltpu.VMEM((2 * ny, 2, 16, 128), F32),
            pltpu.VMEM((2, 2 * ny, 2, 16, 128), F32),
            pltpu.VMEM((2, 8, 16, 128), F32),
            pltpu.VMEM((2, ny, 16, 128), F32),
            pltpu.VMEM((2, nz, 16, 128), F32),
            vec, vec, vec, vec, vec, vec, vec, vec, vec, vec,
            pltpu.VMEM((32, 16), F32),
            dma((n_ag,)), dma((2, 2 * nz)),
            dma((2,)), dma((2, 2)),
            dma((2 * ny - 1,)), dma((2, 2 * ny)),
            dma((7,)), dma((2, 8)),
            dma((ny - 1,)), dma((2, ny)),
            dma((nz - 1,)), dma((2, nz)),
        ],
        compiler_params=pltpu.CompilerParams(
            collective_id=0, has_side_effects=True, vmem_limit_bytes=40 * 1024 * 1024
        ),
    )(
        block_cols,
        counts.reshape(-1),
        rhs.T,
        diagonal.reshape(1, -1),
        blocks,
    )
    return out.T


def solution(mesh):
    sizes = (mesh.shape["rows"] // 4, mesh.shape["cols"] // 2)
    in_specs = (
        P(("rows", "cols"), None),
        P(("rows", "cols")),
        P("rows", "cols", None, None),
        P("rows", "cols"),
        P("rows", "cols"),
    )
    return jax.shard_map(
        functools.partial(per_device, sizes),
        mesh=mesh,
        in_specs=in_specs,
        out_specs=P(("rows", "cols"), None),
        check_vma=False,
    )
```

time: 826 us -> 146 us (0.18); the launches traced: 813 us -> 145 us
  blocking collectives: 336 us -> 0 us
  other arithmetic: 170 us -> 0 us
  Pallas kernels: 0 us -> 140 us
  local copies, waits for them, and re-layouts: 133 us -> 5 us
  waiting for transfers between devices: 83.5 us -> 0 us
  starting transfers between devices: 45 us -> 0 us
  matrix products: 37.5 us -> 0 us
    all_to_all x17 -> x0, blocking collectives: 307 us -> none  [copy_for_each(): lax.all_to_all(jnp.broadcast_to(shard[None], (length, *shard.shape)), axi...]
    pallas_call x0 -> x1, Pallas kernels: none -> 140 us  [per_device(): pl.pallas_call(functools.partial(kernel, sizes), out_shape=jax.ShapeDtype...]
    slice x229 -> x0, local copies, waits for them, and re-layouts: 90.4 us -> none  [the longest x109 68.3 us: solve_block(): pivot_row = joined[index] / joined[index, index]]
    all_to_all x7 -> x0, waiting for transfers between devices: 83.5 us -> none  [copy_for_each(): lax.all_to_all(jnp.broadcast_to(shard[None], (length, *shard.shape)), axi...]
    div x112 -> x0, other arithmetic: 72.2 us -> none  [solve_block(): pivot_row = joined[index] / joined[index, index]]
    mul x105 -> x0, other arithmetic: 67.2 us -> none  [solve_block(): joined = joined - joined[:, index:index + 1] * pivot_row[None, :]]
    all_to_all x7 -> x0, starting transfers between devices: 45 us -> none  [copy_for_each(): lax.all_to_all(jnp.broadcast_to(shard[None], (length, *shard.shape)), axi...]
    dot_general x31 -> x0, matrix products: 37.5 us -> none  [the longest x8 15.1 us: block_rows(): jnp.einsum('rkij,rkjs->ris', blocks, picked, precision=lax.Precision.HIGH...]
  transfers between devices with their start and end apart: 7 -> 0, of which waited for: 7 -> 0; matrix products, arithmetic and copies ran while one was open for 1% -> 0% of each run, Pallas kernels for 0% -> 0%
where the time goes in v1:
time: 146 us; the launch traced here: 145 us
  Pallas kernels  140 us (96%)
  local copies, waits for them, and re-layouts  5 us (3%)
    pallas_call x1, Pallas kernels, per_device(): pl.pallas_call(functools.partial(kernel, sizes), out_shape=jax.ShapeDtype...  140 us
    unnamed x10, local copies, waits for them, and re-layouts  5 us

profile of v1, /device:TPU:1, one launch (start us, length us, event | category | flops | bytes accessed | tf_op | source)
XLA Modules:
  0.0 145.3 jit_solution(6369855395590277429)
XLA Ops:
  0.0 0.8 copy.6.cols_ref
  0.8 0.0 copy-start
  0.8 1.6 %copy-done = f32[16,2,128,128]{3,2,1,0:T(8,128)S(1)} copy-done((f32[16,2,128,128]{3,2,1,0:T(8,128)S(1)}, f32[16,2,128,128]{3,2,1,0:T(8,128)}, u32[]{:S(2)}) %copy-start) | copy-done | bytes 2097176
  2.3 0.0 copy-start.1
  2.3 0.7 copy-done.1
  3.1 0.0 copy-start.2
  3.1 0.7 copy-done.2
  3.7 0.0 copy-start.3
  3.7 0.7 copy-done.3
  4.4 140.3 %shard_map.55 = f32[16,256]{1,0:T(8,128)S(1)} custom-call(s32[16,2]{1,0:T(8,128)S(1)} %copy.6.cols_ref, s32[16]{0:T(128)S(1)} %bitcast.7, f32[16,256]{1,0:T(8,128)S(1)} %bitcast.5, f32[1,256]{1,0:T(1,128)S(1)} %bitcast.6, f32[16,2,128,128]{3,2,1,0:T(8,128)S(1)} %copy-done), custom_call_target="tpu_custom_call" | custom-call | tf_op jit(solution)/shard_map/pallas_call | solution.py:420
  144.7 0.6 copy.8
Async XLA Ops:
  0.8 1.6 %copy-start = (f32[16,2,128,128]{3,2,1,0:T(8,128)S(1)}, f32[16,2,128,128]{3,2,1,0:T(8,128)}, u32[]{:S(2)}) copy-start(f32[16,2,128,128]{3,2,1,0:T(8,128)} %blocks_ref.1) | copy-start | bytes 6291460
  2.3 0.7 copy-start.1
  3.1 0.7 copy-start.2
  3.7 0.7 copy-start.3

commit v2 on v1

v2 whole, which is shorter than its diff:
```python
import functools

import jax
import jax.numpy as jnp
from jax import lax
from jax.experimental import pallas as pl
from jax.experimental.pallas import tpu as pltpu
from jax.sharding import PartitionSpec as P

ITERS = 4
MESH = pl.DeviceIdType.MESH
HIGHEST = lax.Precision.HIGHEST
F32 = jnp.float32
BF16 = jnp.bfloat16
NT = (((1,), (1,)), ((), ()))
NN = (((1,), (0,)), ((), ()))


def mm(a, b, dims=NN):
    return lax.dot_general(a, b, dims, precision=HIGHEST, preferred_element_type=F32)


def kernel(
    sizes,
    cols_ref, counts_ref, rhs_hbm, diag_hbm, blocks_hbm, out_ref,
    rhs_ref, diag_ref, blocks_ref, at, gb0, gb1, prod, rsb, arx, ary, arz,
    sh, pv, sv, zv, vv, rv, wv, tv, qv, xv, at_small,
    in_sem, blk_sem, ag_ssem, ag_rsem, fw_rsem, rs_ssem, rs_rsem,
    ax_ssem, ax_rsem, ay_ssem, ay_rsem, az_ssem, az_rsem,
):
    NZ, NY = sizes
    r = lax.axis_index("rows")
    c = lax.axis_index("cols")
    core = lax.rem(r, 2)
    z = lax.rem(lax.div(r, 2), NZ)
    a = lax.div(r, 2 * NZ)
    xh = lax.div(c, NY)
    y = lax.rem(c, NY)
    x = xh * 2 + a
    n_cols = 2 * NY

    rhs_in = pltpu.make_async_copy(rhs_hbm, rhs_ref, in_sem.at[0])
    diag_in = pltpu.make_async_copy(diag_hbm, diag_ref, in_sem.at[1])
    blocks_in = [
        pltpu.make_async_copy(
            blocks_hbm.at[pl.ds(4 * q, 4)], blocks_ref.at[pl.ds(4 * q, 4)], blk_sem.at[q]
        )
        for q in range(4)
    ]
    rhs_in.start()
    diag_in.start()
    for cp in blocks_in:
        cp.start()

    def device(fx, dy, dz, fk):
        xh_ = (1 - xh) if fx & 2 else xh
        a_ = (1 - a) if fx & 1 else a
        k_ = (1 - core) if fk else core
        y_ = lax.rem(y + dy, NY) if dy else y
        z_ = lax.rem(z + dz, NZ) if dz else z
        return ((a_ * NZ + z_) * 2 + k_, xh_ * NY + y_)

    def slot(fk, fa, dz):
        return ((fk * 2 + fa) * NZ + dz) * 2

    def far(n):
        return lambda d: -min(d, n - d)

    z_order = sorted(range(1, NZ), key=far(NZ))
    y_order = sorted(range(NY), key=far(NY))
    far_z = [d for d in z_order if min(d, NZ - d) >= 3]
    mid_z = [d for d in z_order if min(d, NZ - d) < 3]
    scatter_peers = [(2, dy, 0, 0) for dy in y_order] + [(0, dy, 0, 0) for dy in y_order if dy]
    plane_peers = [(fx, 0, 0, fk) for fx in (2, 3, 1, 0) for fk in (1, 0) if (fx, fk) != (0, 0)]
    y_peers = [(0, dy, 0, 1) for dy in y_order if dy]
    z_peers = [(0, 0, dz, 1) for dz in z_order]
    gather_peers = [(0, 0, dz, 1) for dz in z_order] + [(1, 0, dz, 1) for dz in mid_z]
    gather_peers += [(1, 0, 0, 1), (1, 0, 0, 0), (0, 0, 0, 1)]

    barrier = pltpu.get_barrier_semaphore()
    greet = sorted(set(scatter_peers + plane_peers + y_peers + z_peers + gather_peers))
    for peer in greet:
        pl.semaphore_signal(barrier, inc=1, device_id=device(*peer), device_id_type=MESH)

    def prepare():
        for q in range(4):
            blocks_in[q].wait()

            def some(p, carry):
                for b_ in range(2):
                    b = 4 * q + 2 * p + b_
                    cnt = counts_ref[b]
                    for k in range(2):
                        blk = blocks_ref[b, k]
                        blk = jnp.where(k < cnt, blk, 0.0).T
                        hi = blk.astype(BF16)
                        mid = (blk - hi.astype(F32)).astype(BF16)
                        at[b, k * 128:(k + 1) * 128, 0:128] = hi
                        at[b, k * 128:(k + 1) * 128, 128:256] = mid
                return carry

            lax.fori_loop(0, 2, some, 0)

    rhs_in.wait()
    diag_in.wait()
    rhs = rhs_ref[...]
    sh[...] = rhs
    rv[...] = rhs
    wv[...] = rhs
    zv[...] = rhs
    qv[...] = rhs
    xv[...] = -rhs
    zero = jnp.zeros_like(rhs)
    pv[...] = zero
    sv[...] = zero
    vv[...] = zero
    tv[...] = zero
    row16 = lax.broadcasted_iota(jnp.int32, (16, 128), 0)
    lane16 = lax.broadcasted_iota(jnp.int32, (16, 128), 1)
    eye_at_32 = jnp.where(lane16 == row16 + 32, 1.0, 0.0)
    row32 = lax.broadcasted_iota(jnp.int32, (32, 128), 0)
    lane32 = lax.broadcasted_iota(jnp.int32, (32, 128), 1)
    pick = jnp.where(lane32 == row32 + 16, 1.0, 0.0)
    pad96 = jnp.zeros((96, 256), F32)
    pad112 = jnp.zeros((112, 256), F32)
    at_small[...] = jnp.zeros((32, 16), F32)

    pl.semaphore_wait(barrier, len(greet))

    gbs = (gb0, gb1)

    def arrival(ref, sem):
        pltpu.make_async_remote_copy(
            src_ref=ref, dst_ref=ref, send_sem=ag_ssem.at[0], recv_sem=sem,
            device_id=device(0, 0, 0, 1), device_id_type=MESH,
        ).wait_recv()

    def gather_send(par, sends, src, dst, peer, sem):
        cp = pltpu.make_async_remote_copy(
            src_ref=src, dst_ref=dst, send_sem=ag_ssem.at[len(sends)], recv_sem=sem,
            device_id=device(*peer), device_id_type=MESH,
        )
        cp.start()
        sends.append(cp)

    def gather_start(par, vec, sends):
        gb = gbs[par]
        if vec is not None:
            gb[0] = vec[:, 0:128]
            gb[1] = vec[:, 128:256]
        own = gb.at[pl.ds(0, 2)]

        def send(fk, fa, dz):
            s = slot(fk, fa, (NZ - dz) % NZ)
            gather_send(
                par, sends, own, gb.at[pl.ds(s, 2)], (fa, 0, dz, fk), ag_rsem.at[par, s // 2]
            )

        if vec is not None:
            for dz in far_z:
                send(1, 0, dz)
            send(1, 0, 0)
            return
        for dz in mid_z:
            for fa in (1, 0):
                send(1, fa, dz)
        send(1, 1, 0)
        send(0, 1, 0)

    def gather_parts(par, sends, part):
        gb = gbs[par]

        def place(fk, fa, dz, n=1):
            return gb.at[pl.ds(slot(fk, fa, dz), 2 * n)]

        def sem(fk, fa, dz):
            return ag_rsem.at[par, slot(fk, fa, dz) // 2]

        lo, n_far = min(far_z), len(far_z)
        for d in far_z if part == 0 else ():
            dz = NZ - d
            arrival(place(1, 0, dz), sem(1, 0, dz))
            gather_send(par, sends, place(1, 0, dz), place(1, 1, dz), (1, 0, 0, 0), sem(1, 1, dz))
            gather_send(par, sends, place(1, 0, dz), place(0, 1, dz), (1, 0, 0, 1), sem(0, 1, dz))
        if part == 0:
            gather_send(
                par, sends, place(1, 0, lo, n_far), place(0, 0, lo, n_far),
                (0, 0, 0, 1), fw_rsem.at[par]
            )
        for d in mid_z if part == 1 else ():
            dz = NZ - d
            for fa in (0, 1):
                arrival(place(1, fa, dz), sem(1, fa, dz))
                gather_send(
                    par, sends, place(1, fa, dz), place(0, fa, dz), (0, 0, 0, 1), sem(0, fa, dz)
                )
        if part < 2:
            return
        arrival(place(1, 0, 0), sem(1, 0, 0))
        arrival(place(1, 1, 0), sem(1, 1, 0))
        arrival(place(0, 1, 0), sem(0, 1, 0))
        arrival(place(0, 0, lo, n_far), fw_rsem.at[par])
        for d in mid_z:
            dz = NZ - d
            for fa in (0, 1):
                arrival(place(0, fa, dz), sem(0, fa, dz))
        for d in far_z:
            dz = NZ - d
            arrival(place(1, 1, dz), sem(1, 1, dz))
            arrival(place(0, 1, dz), sem(0, 1, dz))

    def block_row(gb, b):
        parts = []
        for k in range(2):
            l = cols_ref[k, b]
            fk = ((l >> 1) & 1) ^ core
            dz = ((l >> 2) + NZ - z) & (NZ - 1)
            fa = (l // (4 * NZ)) ^ a
            parts.append(gb[slot(fk, fa, dz) + (l & 1)])
        v = jnp.concatenate(parts, axis=1)
        vh = v.astype(BF16)
        vm = (v - vh.astype(F32)).astype(BF16)
        both = jnp.concatenate([vh, vm], axis=0)
        full = lax.dot_general(both, at[b], NN, preferred_element_type=F32)
        return full[0:16, 0:128] + (full[16:32, 0:128] + full[0:16, 128:256])

    def products(par):
        gb = gbs[par]
        sends = []
        for n, peer in enumerate(scatter_peers + [(0, 0, 0, 0)]):
            c_ = device(*peer)[1]
            for h in range(2):
                prod[c_, h] = block_row(gb, c_ * 2 + h)
            if n < len(scatter_peers):
                cp = pltpu.make_async_remote_copy(
                    src_ref=prod.at[c_],
                    dst_ref=rsb.at[par, c],
                    send_sem=rs_ssem.at[n],
                    recv_sem=rs_rsem.at[par, c],
                    device_id=device(*peer),
                    device_id_type=MESH,
                )
                cp.start()
                sends.append(cp)
        return sends

    def scatter_finish(par, vec):
        own = prod[c]
        total = jnp.concatenate([own[0], own[1]], axis=1) + diag_ref[...] * vec
        for peer in reversed(scatter_peers):
            c_ = device(*peer)[1]
            pltpu.make_async_remote_copy(
                src_ref=prod.at[c_],
                dst_ref=rsb.at[par, c_],
                send_sem=rs_ssem.at[0],
                recv_sem=rs_rsem.at[par, c_],
                device_id=device(*peer),
                device_id_type=MESH,
            ).wait_recv()
            got = rsb[par, c_]
            total = total + jnp.concatenate([got[0], got[1]], axis=1)
        return total

    def spread(par, part, buf, mine, peers, ssem, rsem):
        buf[par, mine] = part
        sends = []
        for n, peer in enumerate(peers):
            cp = pltpu.make_async_remote_copy(
                src_ref=buf.at[par, mine], dst_ref=buf.at[par, mine],
                send_sem=ssem.at[n], recv_sem=rsem.at[par, mine],
                device_id=device(*peer), device_id_type=MESH,
            )
            cp.start()
            sends.append(cp)
        return sends

    def collect(par, buf, index_of, peers, ssem, rsem):
        for peer in reversed(peers):
            there = index_of(*device(*peer))
            pltpu.make_async_remote_copy(
                src_ref=buf.at[par, there], dst_ref=buf.at[par, there],
                send_sem=ssem.at[0], recv_sem=rsem.at[par, there],
                device_id=device(*peer), device_id_type=MESH,
            ).wait_recv()
        parts = [buf[par, n] for n in range(buf.shape[1])]
        while len(parts) > 1:
            parts = [parts[n] + parts[n + 1] for n in range(0, len(parts), 2)]
        return parts[0]

    def plane_index(r_, c_):
        return (lax.div(c_, NY) * 2 + lax.div(r_, 2 * NZ)) * 2 + lax.rem(r_, 2)

    def y_index(r_, c_):
        return lax.rem(c_, NY)

    def z_index(r_, c_):
        return lax.rem(lax.div(r_, 2), NZ)

    in_plane = (arx, plane_index, plane_peers, ax_ssem, ax_rsem)
    in_y = (ary, y_index, y_peers, ay_ssem, ay_rsem)
    in_z = (arz, z_index, z_peers, az_ssem, az_rsem)

    def reduce_first(par, part):
        buf, index_of, peers, ssem, rsem = in_y
        return spread(par, part, buf, index_of(r, c), peers, ssem, rsem)

    def reduce_second(par):
        part = collect(par, *in_y)
        buf, index_of, peers, ssem, rsem = in_plane
        return spread(par, part, buf, index_of(r, c), peers, ssem, rsem)

    def reduce_third(par):
        part = collect(par, *in_plane)
        buf, index_of, peers, ssem, rsem = in_z
        return spread(par, part, buf, index_of(r, c), peers, ssem, rsem)

    def reduce_finish(par):
        return collect(par, *in_z)

    def drain(sends):
        for cp in sends:
            cp.wait_send()

    def omega_part():
        yy = wv[...] - mm(at_small[0:16, :], zv[...])
        return yy

    def sums_of(yy, qq):
        d = mm(yy, jnp.concatenate([sh[...], pad112], axis=0), NT)
        along = jnp.sum(yy * qq, axis=1, keepdims=True)
        square = jnp.sum(yy * yy, axis=1, keepdims=True)
        return jnp.where(lane16 == 16, along, jnp.where(lane16 == 17, square, d))

    def omega_of(total):
        along = jnp.sum(jnp.where(lane16 == 16, total, 0.0), keepdims=True)
        square = jnp.sum(jnp.where(lane16 == 17, total, 0.0), keepdims=True)
        return along / square

    def solve(total):
        joined = jnp.where(lane16 < 32, total, eye_at_32)
        for i in range(16):
            pivot_row = joined[i:i + 1, :] / joined[i:i + 1, i:i + 1]
            column = joined[:, i:i + 1]
            joined = jnp.where(row16 == i, pivot_row, joined - column * pivot_row)
        return mm(pick, joined, NT)

    def step(i, carry):
        first = i == 0
        par = 0
        ag = []
        gather_start(par, zv[...], ag)
        yy = jnp.where(first, 0.0, wv[...] - mm(at_small[0:16, :], zv[...]))
        qq = qv[...]
        ax = reduce_first(par, sums_of(yy, qq))
        gather_start(par, None, ag)
        pl.when(first)(prepare)
        ay = reduce_second(par)
        gather_parts(par, ag, 0)
        az = reduce_third(par)
        gather_parts(par, ag, 1)
        gather_parts(par, ag, 2)
        rs = products(par)
        total = reduce_finish(par)
        omega = jnp.where(first, 1.0, omega_of(total))
        beta_t = jnp.where(first, 0.0, -mm(total[:, 0:16], at_small[16:32, :]))
        alpha_t = at_small[0:16, :]
        xv[...] = xv[...] + mm(alpha_t, pv[...]) + omega * qq
        res = qq - omega * yy
        new_p = res + mm(beta_t, pv[...] - omega * sv[...])
        kept = mm(beta_t, sv[...] - omega * zv[...])
        left = yy - omega * tv[...]
        vv[...] = scatter_finish(par, zv[...])
        w_new = jnp.where(first, vv[...], left + omega * mm(alpha_t, vv[...]))
        drain(ag + ax + ay + az + rs)
        par = 1
        ag = []
        gather_start(par, w_new, ag)
        s_new = w_new + kept
        d = mm(sh[...], jnp.concatenate([s_new, res, pad96], axis=0), NT)
        ax = reduce_first(par, d)
        gather_start(par, None, ag)
        wv[...] = w_new
        pv[...] = new_p
        sv[...] = s_new
        ay = reduce_second(par)
        gather_parts(par, ag, 0)
        az = reduce_third(par)
        gather_parts(par, ag, 1)
        gather_parts(par, ag, 2)
        rs = products(par)
        total = reduce_finish(par)
        at_small[...] = solve(total)
        qv[...] = res - mm(at_small[0:16, :], s_new)
        u = mm(beta_t, zv[...] - omega * vv[...])
        t_new = scatter_finish(par, w_new)
        tv[...] = t_new
        zv[...] = jnp.where(first, t_new, t_new + u)
        drain(ag + ax + ay + az + rs)
        return carry

    lax.fori_loop(0, ITERS, step, 0)

    par = 0
    qq = qv[...]
    yy = wv[...] - mm(at_small[0:16, :], zv[...])
    ax = reduce_first(par, sums_of(yy, qq))
    partial = xv[...] + mm(at_small[0:16, :], pv[...])
    ay = reduce_second(par)
    az = reduce_third(par)
    total = reduce_finish(par)
    out_ref[...] = partial + omega_of(total) * qq
    drain(ax + ay + az)


def per_device(sizes, rhs, diagonal, blocks, block_cols, counts):
    nz, ny = sizes
    vm = pl.BlockSpec(memory_space=pltpu.VMEM)
    hbm = pl.BlockSpec(memory_space=pl.ANY)
    sm = pl.BlockSpec(memory_space=pltpu.SMEM)
    vec = pltpu.VMEM((16, 256), F32)
    dma = pltpu.SemaphoreType.DMA
    out = pl.pallas_call(
        functools.partial(kernel, sizes),
        out_shape=jax.ShapeDtypeStruct((16, 256), F32),
        in_specs=[sm, sm, hbm, hbm, hbm],
        out_specs=vm,
        scratch_shapes=[
            vec,
            pltpu.VMEM((1, 256), F32),
            pltpu.VMEM((16, 2, 128, 128), F32),
            pltpu.VMEM((16, 256, 256), BF16),
            pltpu.VMEM((8 * nz, 16, 128), F32),
            pltpu.VMEM((8 * nz, 16, 128), F32),
            pltpu.VMEM((2 * ny, 2, 16, 128), F32),
            pltpu.VMEM((2, 2 * ny, 2, 16, 128), F32),
            pltpu.VMEM((2, 8, 16, 128), F32),
            pltpu.VMEM((2, ny, 16, 128), F32),
            pltpu.VMEM((2, nz, 16, 128), F32),
            vec, vec, vec, vec, vec, vec, vec, vec, vec, vec,
            pltpu.VMEM((32, 16), F32),
            dma((2,)), dma((4,)),
            dma((40,)), dma((2, 4 * nz)), dma((2,)),
            dma((2 * ny - 1,)), dma((2, 2 * ny)),
            dma((7,)), dma((2, 8)),
            dma((ny - 1,)), dma((2, ny)),
            dma((nz - 1,)), dma((2, nz)),
        ],
        compiler_params=pltpu.CompilerParams(
            collective_id=0, has_side_effects=True, vmem_limit_bytes=60 * 1024 * 1024
        ),
    )(
        block_cols.T,
        counts.reshape(-1),
        rhs.T,
        diagonal.reshape(1, -1),
        blocks,
    )
    return out.T


def solution(mesh):
    sizes = (mesh.shape["rows"] // 4, mesh.shape["cols"] // 2)
    in_specs = (
        P(("rows", "cols"), None),
        P(("rows", "cols")),
        P("rows", "cols", None, None),
        P("rows", "cols"),
        P("rows", "cols"),
    )
    return jax.shard_map(
        functools.partial(per_device, sizes),
        mesh=mesh,
        in_specs=in_specs,
        out_specs=P(("rows", "cols"), None),
        check_vma=False,
    )
```

time: 146 us -> 137 us (0.938)
  Pallas kernels: 140 us -> 135 us
  local copies, waits for them, and re-layouts: 5 us -> 1.32 us
    pallas_call x1, Pallas kernels: 140 us -> 135 us  [per_device(): pl.pallas_call(functools.partial(kernel, sizes), out_shape=jax.ShapeDtype...]
    unnamed x10 -> x1, local copies, waits for them, and re-layouts: 5 us -> 1.32 us
where the time goes in v2:
time: 137 us
  Pallas kernels  135 us (99%)
    pallas_call x1, Pallas kernels, per_device(): pl.pallas_call(functools.partial(kernel, sizes), out_shape=jax.ShapeDtype...  135 us

profile of v2, /device:TPU:1, one launch (start us, length us, event | category | flops | bytes accessed | tf_op | source)
XLA Modules:
  0.0 136.7 jit_solution(2247647502611144232)
XLA Ops:
  0.0 135.4 %shard_map.55 = f32[16,256]{1,0:T(8,128)} custom-call(s32[2,16]{1,0:T(2,128)} %bitcast.7, s32[16]{0:T(128)} %bitcast.9, f32[16,256]{1,0:T(8,128)} %bitcast.6, f32[1,256]{1,0:T(1,128)} %bitcast.8, f32[16,2,128,128]{3,2,1,0:T(8,128)} %blocks_hbm.1), custom_call_target="tpu_custom_call" | custom-call | tf_op jit(solution)/shard_map/pallas_call | solution.py:422
  135.4 1.3 copy.7

commit v3 on v2

--- a/solution.py
+++ b/solution.py
@@ -125,6 +125,7 @@
     pad112 = jnp.zeros((112, 256), F32)
     at_small[...] = jnp.zeros((32, 16), F32)
 
+    prepare()
     pl.semaphore_wait(barrier, len(greet))
 
     gbs = (gb0, gb1)
@@ -353,7 +354,6 @@
         qq = qv[...]
         ax = reduce_first(par, sums_of(yy, qq))
         gather_start(par, None, ag)
-        pl.when(first)(prepare)
         ay = reduce_second(par)
         gather_parts(par, ag, 0)
         az = reduce_third(par)
@@ -369,9 +369,9 @@
         new_p = res + mm(beta_t, pv[...] - omega * sv[...])
         kept = mm(beta_t, sv[...] - omega * zv[...])
         left = yy - omega * tv[...]
+        drain(ag + ax + ay + az + rs)
         vv[...] = scatter_finish(par, zv[...])
         w_new = jnp.where(first, vv[...], left + omega * mm(alpha_t, vv[...]))
-        drain(ag + ax + ay + az + rs)
         par = 1
         ag = []
         gather_start(par, w_new, ag)
@@ -392,10 +392,10 @@
         at_small[...] = solve(total)
         qv[...] = res - mm(at_small[0:16, :], s_new)
         u = mm(beta_t, zv[...] - omega * vv[...])
+        drain(ag + ax + ay + az + rs)
         t_new = scatter_finish(par, w_new)
         tv[...] = t_new
         zv[...] = jnp.where(first, t_new, t_new + u)
-        drain(ag + ax + ay + az + rs)
         return carry
 
     lax.fori_loop(0, ITERS, step, 0)

time: 137 us -> 135 us (0.985)
  no operation moved by 1% of the time
where the time goes in v3:
time: 135 us
  Pallas kernels  134 us (99%)
    pallas_call x1, Pallas kernels, per_device(): pl.pallas_call(functools.partial(kernel, sizes), out_shape=jax.ShapeDtype...  134 us

profile of v3, /device:TPU:1, one launch (start us, length us, event | category | flops | bytes accessed | tf_op | source)
XLA Modules:
  0.0 135.4 jit_solution(17839099644914105891)
XLA Ops:
  0.0 134.0 %shard_map.55 = f32[16,256]{1,0:T(8,128)} custom-call(s32[2,16]{1,0:T(2,128)} %bitcast.7, s32[16]{0:T(128)} %bitcast.9, f32[16,256]{1,0:T(8,128)} %bitcast.6, f32[1,256]{1,0:T(1,128)} %bitcast.8, f32[16,2,128,128]{3,2,1,0:T(8,128)} %blocks_hbm.1), custom_call_target="tpu_custom_call" | custom-call | tf_op jit(solution)/shard_map/pallas_call | solution.py:422
  134.0 1.3 copy.7

commit v4 on v3

--- a/solution.py
+++ b/solution.py
@@ -68,17 +68,17 @@
 
     z_order = sorted(range(1, NZ), key=far(NZ))
     y_order = sorted(range(NY), key=far(NY))
-    far_z = [d for d in z_order if min(d, NZ - d) >= 3]
-    mid_z = [d for d in z_order if min(d, NZ - d) < 3]
+    far_z = [d for d in z_order if min(d, NZ - d) >= 4]
+    mid_z = [d for d in z_order if min(d, NZ - d) < 4]
     scatter_peers = [(2, dy, 0, 0) for dy in y_order] + [(0, dy, 0, 0) for dy in y_order if dy]
-    plane_peers = [(fx, 0, 0, fk) for fx in (2, 3, 1, 0) for fk in (1, 0) if (fx, fk) != (0, 0)]
-    y_peers = [(0, dy, 0, 1) for dy in y_order if dy]
+    chip_peers = [(0, 0, 0, 1)]
+    plane_peers = [(fx, dy, 0, 1) for fx in (2, 3, 1, 0) for dy in y_order if (fx, dy) != (0, 0)]
     z_peers = [(0, 0, dz, 1) for dz in z_order]
     gather_peers = [(0, 0, dz, 1) for dz in z_order] + [(1, 0, dz, 1) for dz in mid_z]
     gather_peers += [(1, 0, 0, 1), (1, 0, 0, 0), (0, 0, 0, 1)]
 
     barrier = pltpu.get_barrier_semaphore()
-    greet = sorted(set(scatter_peers + plane_peers + y_peers + z_peers + gather_peers))
+    greet = sorted(set(scatter_peers + plane_peers + z_peers + gather_peers))
     for peer in greet:
         pl.semaphore_signal(barrier, inc=1, device_id=device(*peer), device_id_type=MESH)
 
@@ -160,9 +160,12 @@
         if vec is not None:
             for dz in far_z:
                 send(1, 0, dz)
+            for dz in mid_z[:2]:
+                for fa in (1, 0):
+                    send(1, fa, dz)
             send(1, 0, 0)
             return
-        for dz in mid_z:
+        for dz in mid_z[2:]:
             for fa in (1, 0):
                 send(1, fa, dz)
         send(1, 1, 0)
@@ -288,25 +291,25 @@
             parts = [parts[n] + parts[n + 1] for n in range(0, len(parts), 2)]
         return parts[0]
 
+    def chip_index(r_, c_):
+        return lax.rem(r_, 2)
+
     def plane_index(r_, c_):
-        return (lax.div(c_, NY) * 2 + lax.div(r_, 2 * NZ)) * 2 + lax.rem(r_, 2)
-
-    def y_index(r_, c_):
-        return lax.rem(c_, NY)
+        return (lax.div(c_, NY) * 2 + lax.div(r_, 2 * NZ)) * NY + lax.rem(c_, NY)
 
     def z_index(r_, c_):
         return lax.rem(lax.div(r_, 2), NZ)
 
     in_plane = (arx, plane_index, plane_peers, ax_ssem, ax_rsem)
-    in_y = (ary, y_index, y_peers, ay_ssem, ay_rsem)
+    in_chip = (ary, chip_index, chip_peers, ay_ssem, ay_rsem)
     in_z = (arz, z_index, z_peers, az_ssem, az_rsem)
 
     def reduce_first(par, part):
-        buf, index_of, peers, ssem, rsem = in_y
+        buf, index_of, peers, ssem, rsem = in_chip
         return spread(par, part, buf, index_of(r, c), peers, ssem, rsem)
 
     def reduce_second(par):
-        part = collect(par, *in_y)
+        part = collect(par, *in_chip)
         buf, index_of, peers, ssem, rsem = in_plane
         return spread(par, part, buf, index_of(r, c), peers, ssem, rsem)
 
@@ -356,8 +359,8 @@
         gather_start(par, None, ag)
         ay = reduce_second(par)
         gather_parts(par, ag, 0)
+        gather_parts(par, ag, 1)
         az = reduce_third(par)
-        gather_parts(par, ag, 1)
         gather_parts(par, ag, 2)
         rs = products(par)
         total = reduce_finish(par)
@@ -384,8 +387,8 @@
         sv[...] = s_new
         ay = reduce_second(par)
         gather_parts(par, ag, 0)
+        gather_parts(par, ag, 1)
         az = reduce_third(par)
-        gather_parts(par, ag, 1)
         gather_parts(par, ag, 2)
         rs = products(par)
         total = reduce_finish(par)
@@ -433,16 +436,16 @@
             pltpu.VMEM((8 * nz, 16, 128), F32),
             pltpu.VMEM((2 * ny, 2, 16, 128), F32),
             pltpu.VMEM((2, 2 * ny, 2, 16, 128), F32),
-            pltpu.VMEM((2, 8, 16, 128), F32),
-            pltpu.VMEM((2, ny, 16, 128), F32),
+            pltpu.VMEM((2, 4 * ny, 16, 128), F32),
+            pltpu.VMEM((2, 2, 16, 128), F32),
             pltpu.VMEM((2, nz, 16, 128), F32),
             vec, vec, vec, vec, vec, vec, vec, vec, vec, vec,
             pltpu.VMEM((32, 16), F32),
             dma((2,)), dma((4,)),
             dma((40,)), dma((2, 4 * nz)), dma((2,)),
             dma((2 * ny - 1,)), dma((2, 2 * ny)),
-            dma((7,)), dma((2, 8)),
-            dma((ny - 1,)), dma((2, ny)),
+            dma((4 * ny - 1,)), dma((2, 4 * ny)),
+            dma((1,)), dma((2, 2)),
             dma((nz - 1,)), dma((2, nz)),
         ],
         compiler_params=pltpu.CompilerParams(

time: 135 us -> 133 us (0.985)
  Pallas kernels: 134 us -> 132 us
    pallas_call x1, Pallas kernels: 134 us -> 132 us  [per_device(): pl.pallas_call(functools.partial(kernel, sizes), out_shape=jax.ShapeDtype...]
where the time goes in v4:
time: 133 us
  Pallas kernels  132 us (99%)
    pallas_call x1, Pallas kernels, per_device(): pl.pallas_call(functools.partial(kernel, sizes), out_shape=jax.ShapeDtype...  132 us

profile of v4, /device:TPU:1, one launch (start us, length us, event | category | flops | bytes accessed | tf_op | source)
XLA Modules:
  0.0 133.2 jit_solution(17890759645531039652)
XLA Ops:
  0.0 131.9 %shard_map.55 = f32[16,256]{1,0:T(8,128)} custom-call(s32[2,16]{1,0:T(2,128)} %bitcast.7, s32[16]{0:T(128)} %bitcast.9, f32[16,256]{1,0:T(8,128)} %bitcast.6, f32[1,256]{1,0:T(1,128)} %bitcast.8, f32[16,2,128,128]{3,2,1,0:T(8,128)} %blocks_hbm.1), custom_call_target="tpu_custom_call" | custom-call | tf_op jit(solution)/shard_map/pallas_call | solution.py:425
  131.9 1.3 copy.7

commit v5 on v4

--- a/solution.py
+++ b/solution.py
@@ -266,11 +266,12 @@
         return total
 
     def spread(par, part, buf, mine, peers, ssem, rsem):
-        buf[par, mine] = part
+        rows = part.shape[0]
+        buf[par, mine, 0:rows] = part
         sends = []
         for n, peer in enumerate(peers):
             cp = pltpu.make_async_remote_copy(
-                src_ref=buf.at[par, mine], dst_ref=buf.at[par, mine],
+                src_ref=buf.at[par, mine, pl.ds(0, rows)], dst_ref=buf.at[par, mine, pl.ds(0, rows)],
                 send_sem=ssem.at[n], recv_sem=rsem.at[par, mine],
                 device_id=device(*peer), device_id_type=MESH,
             )
@@ -278,15 +279,15 @@
             sends.append(cp)
         return sends
 
-    def collect(par, buf, index_of, peers, ssem, rsem):
+    def collect(par, rows, buf, index_of, peers, ssem, rsem):
         for peer in reversed(peers):
             there = index_of(*device(*peer))
             pltpu.make_async_remote_copy(
-                src_ref=buf.at[par, there], dst_ref=buf.at[par, there],
+                src_ref=buf.at[par, there, pl.ds(0, rows)], dst_ref=buf.at[par, there, pl.ds(0, rows)],
                 send_sem=ssem.at[0], recv_sem=rsem.at[par, there],
                 device_id=device(*peer), device_id_type=MESH,
             ).wait_recv()
-        parts = [buf[par, n] for n in range(buf.shape[1])]
+        parts = [buf[par, n, 0:rows] for n in range(buf.shape[1])]
         while len(parts) > 1:
             parts = [parts[n] + parts[n + 1] for n in range(0, len(parts), 2)]
         return parts[0]
@@ -308,18 +309,18 @@
         buf, index_of, peers, ssem, rsem = in_chip
         return spread(par, part, buf, index_of(r, c), peers, ssem, rsem)
 
-    def reduce_second(par):
-        part = collect(par, *in_chip)
+    def reduce_second(par, rows=16):
+        part = collect(par, rows, *in_chip)
         buf, index_of, peers, ssem, rsem = in_plane
         return spread(par, part, buf, index_of(r, c), peers, ssem, rsem)
 
-    def reduce_third(par):
-        part = collect(par, *in_plane)
+    def reduce_third(par, rows=16):
+        part = collect(par, rows, *in_plane)
         buf, index_of, peers, ssem, rsem = in_z
         return spread(par, part, buf, index_of(r, c), peers, ssem, rsem)
 
-    def reduce_finish(par):
-        return collect(par, *in_z)
+    def reduce_finish(par, rows=16):
+        return collect(par, rows, *in_z)
 
     def drain(sends):
         for cp in sends:
@@ -336,8 +337,9 @@
         return jnp.where(lane16 == 16, along, jnp.where(lane16 == 17, square, d))
 
     def omega_of(total):
-        along = jnp.sum(jnp.where(lane16 == 16, total, 0.0), keepdims=True)
-        square = jnp.sum(jnp.where(lane16 == 17, total, 0.0), keepdims=True)
+        lane = lane16[0:total.shape[0], :]
+        along = jnp.sum(jnp.where(lane == 16, total, 0.0), keepdims=True)
+        square = jnp.sum(jnp.where(lane == 17, total, 0.0), keepdims=True)
         return along / square
 
     def solve(total):
@@ -374,7 +376,7 @@
         left = yy - omega * tv[...]
         drain(ag + ax + ay + az + rs)
         vv[...] = scatter_finish(par, zv[...])
-        w_new = jnp.where(first, vv[...], left + omega * mm(alpha_t, vv[...]))
+        w_new = jnp.where(first, vv[...], left + mm(omega * alpha_t, vv[...]))
         par = 1
         ag = []
         gather_start(par, w_new, ag)
@@ -406,11 +408,18 @@
     par = 0
     qq = qv[...]
     yy = wv[...] - mm(at_small[0:16, :], zv[...])
-    ax = reduce_first(par, sums_of(yy, qq))
+
+    def eight(product):
+        folded = product[:, 0:128] + product[:, 128:256]
+        return jnp.sum(folded[0:8, :] + folded[8:16, :], axis=1, keepdims=True)
+
+    lane8 = lane16[0:8, :]
+    part = jnp.where(lane8 == 16, eight(yy * qq), jnp.where(lane8 == 17, eight(yy * yy), 0.0))
+    ax = reduce_first(par, part)
     partial = xv[...] + mm(at_small[0:16, :], pv[...])
-    ay = reduce_second(par)
-    az = reduce_third(par)
-    total = reduce_finish(par)
+    ay = reduce_second(par, 8)
+    az = reduce_third(par, 8)
+    total = reduce_finish(par, 8)
     out_ref[...] = partial + omega_of(total) * qq
     drain(ax + ay + az)
 

time: 133 us -> 133 us (level)
  no operation moved by 1% of the time
where the time goes in v5:
time: 133 us
  Pallas kernels  131 us (98%)
    pallas_call x1, Pallas kernels, per_device(): pl.pallas_call(functools.partial(kernel, sizes), out_shape=jax.ShapeDtype...  131 us

profile of v5, /device:TPU:1, one launch (start us, length us, event | category | flops | bytes accessed | tf_op | source)
XLA Modules:
  0.0 132.7 jit_solution(14820818356075202200)
XLA Ops:
  0.0 131.4 %shard_map.55 = f32[16,256]{1,0:T(8,128)} custom-call(s32[2,16]{1,0:T(2,128)} %bitcast.7, s32[16]{0:T(128)} %bitcast.9, f32[16,256]{1,0:T(8,128)} %bitcast.6, f32[1,256]{1,0:T(1,128)} %bitcast.8, f32[16,2,128,128]{3,2,1,0:T(8,128)} %blocks_hbm.1), custom_call_target="tpu_custom_call" | custom-call | tf_op jit(solution)/shard_map/pallas_call | solution.py:434
  131.4 1.3 copy.7

commit v6 on v5

--- a/solution.py
+++ b/solution.py
@@ -305,6 +305,12 @@
     in_chip = (ary, chip_index, chip_peers, ay_ssem, ay_rsem)
     in_z = (arz, z_index, z_peers, az_ssem, az_rsem)
 
+    def packed(part):
+        return part[0:8, :] + pltpu.roll(part[8:16, :], 64, 1)
+
+    def unpacked(total):
+        return jnp.concatenate([total, pltpu.roll(total, 64, 1)], axis=0)
+
     def reduce_first(par, part):
         buf, index_of, peers, ssem, rsem = in_chip
         return spread(par, part, buf, index_of(r, c), peers, ssem, rsem)
@@ -357,15 +363,15 @@
         gather_start(par, zv[...], ag)
         yy = jnp.where(first, 0.0, wv[...] - mm(at_small[0:16, :], zv[...]))
         qq = qv[...]
-        ax = reduce_first(par, sums_of(yy, qq))
+        ax = reduce_first(par, packed(sums_of(yy, qq)))
         gather_start(par, None, ag)
-        ay = reduce_second(par)
+        ay = reduce_second(par, 8)
         gather_parts(par, ag, 0)
         gather_parts(par, ag, 1)
-        az = reduce_third(par)
+        az = reduce_third(par, 8)
         gather_parts(par, ag, 2)
         rs = products(par)
-        total = reduce_finish(par)
+        total = unpacked(reduce_finish(par, 8))
         omega = jnp.where(first, 1.0, omega_of(total))
         beta_t = jnp.where(first, 0.0, -mm(total[:, 0:16], at_small[16:32, :]))
         alpha_t = at_small[0:16, :]
@@ -382,18 +388,18 @@
         gather_start(par, w_new, ag)
         s_new = w_new + kept
         d = mm(sh[...], jnp.concatenate([s_new, res, pad96], axis=0), NT)
-        ax = reduce_first(par, d)
+        ax = reduce_first(par, packed(d))
         gather_start(par, None, ag)
         wv[...] = w_new
         pv[...] = new_p
         sv[...] = s_new
-        ay = reduce_second(par)
+        ay = reduce_second(par, 8)
         gather_parts(par, ag, 0)
         gather_parts(par, ag, 1)
-        az = reduce_third(par)
+        az = reduce_third(par, 8)
         gather_parts(par, ag, 2)
         rs = products(par)
-        total = reduce_finish(par)
+        total = unpacked(reduce_finish(par, 8))
         at_small[...] = solve(total)
         qv[...] = res - mm(at_small[0:16, :], s_new)
         u = mm(beta_t, zv[...] - omega * vv[...])

time: 133 us -> 131 us (0.985)
    pallas_call x1, Pallas kernels: 131 us -> 130 us  [per_device(): pl.pallas_call(functools.partial(kernel, sizes), out_shape=jax.ShapeDtype...]
where the time goes in v6:
time: 131 us
  Pallas kernels  130 us (99%)
  local copies, waits for them, and re-layouts  1.32 us (1%)
    pallas_call x1, Pallas kernels, per_device(): pl.pallas_call(functools.partial(kernel, sizes), out_shape=jax.ShapeDtype...  130 us

profile of v6, /device:TPU:1, one launch (start us, length us, event | category | flops | bytes accessed | tf_op | source)
XLA Modules:
  0.0 131.3 jit_solution(14056133961717168245)
XLA Ops:
  0.0 129.9 %shard_map.55 = f32[16,256]{1,0:T(8,128)} custom-call(s32[2,16]{1,0:T(2,128)} %bitcast.7, s32[16]{0:T(128)} %bitcast.9, f32[16,256]{1,0:T(8,128)} %bitcast.6, f32[1,256]{1,0:T(1,128)} %bitcast.8, f32[16,2,128,128]{3,2,1,0:T(8,128)} %blocks_hbm.1), custom_call_target="tpu_custom_call" | custom-call | tf_op jit(solution)/shard_map/pallas_call | solution.py:440
  130.0 1.3 %copy.7 = f32[256,16]{0,1:T(8,128)} copy(f32[256,16]{0,1:T(8,128)} %bitcast.5) | data formatting | bytes 32768
